TPU v7x, 32 devices: a whole 2x2x4 slice. The times are simulated.
32 devices in a mesh: band: 2 (over x), vis: 16 (over z, y, core).
Axes of the slice: x: 2, y: 2, z: 4, core: 2. Of those that a mesh axis runs over, the one named last changes fastest.
Arguments:
- sky_image: float32 [4096, 4096], P(('band', 'vis')), as said below
- coef_dual: float32 [4, 2048, 2048], P(None, ('band', 'vis')), may hold values from -12 to 12
- vis_dual: float32 [2, 16, 16, 4, 2, 32], P('band', 'vis'), may hold values from -12 to 12
- visibilities: float32 [2, 16, 16, 4, 2, 32], P('band', 'vis')
- kernel_blocks: bfloat16 [2, 16, 16, 4, 2, 32, 256], P('band', 'vis'), may hold values from -0.375 to 0.375
- tile_rows: int32 [2, 16, 16, 4], P('band', 'vis'), may hold values from 0 to 2047
- tile_counts: int32 [2, 16, 16], P('band', 'vis'), may hold values from 1 to 4, as said below
Outputs:
- new_image: float32 [4096, 4096], P(('band', 'vis'))
- new_coef_dual: float32 [4, 2048, 2048], P(None, ('band', 'vis'))
- new_vis_dual: float32 [2, 16, 16, 4, 2, 32], P('band', 'vis')
Inputs may be any that keep to these rules, and one draw needn't show every extreme that they name: `sky_image`: nonnegative. `tile_counts`: in every band some owner q has all 4 slots live from every device of that band.
All inputs are finite; a program needn't handle non-finite values.
Results may differ from a plain program's by a relative error of at most 0.0018.
Values may be sent and summed in bfloat16 or wider, within the bound.
A program may use at most 128 MiB of HBM per device.

v0:
```python
import math
import jax
import jax.numpy as jnp
from jax import lax
from jax.sharding import PartitionSpec as P

IMG = 4096
low_taps = (
    -0.010597401784997278,
    0.032883011666982945,
    0.030841381835986965,
    -0.18703481171888114,
    -0.02798376941698385,
    0.6308807679295904,
    0.7148465705525415,
    0.23037781330885523,
)
high_taps = tuple(((-1.0) ** offset * low_taps[7 - offset] for offset in range(8)))
highest = lax.Precision.HIGHEST


def shifted(block, axis, distance):
    devices = range(lax.axis_size(axis))
    route = [((i - distance) % len(devices), i) for i in devices]
    return lax.ppermute(block, axis, route)


def dft_table(table_size, sign):
    positions = jnp.arange(table_size, dtype=jnp.int32)
    phase = positions[:, None] * positions[None, :] % table_size
    angle = 2.0 * math.pi / table_size * phase.astype(jnp.float32)
    return (jnp.cos(angle), sign * jnp.sin(angle))


def section_one(table, values):
    return jnp.einsum("kn,...nm->...km", table, values, precision=highest)


def section_two(table, values):
    return jnp.einsum("qm,...km->...qk", table, values, precision=highest)


def dft_last(real_in, imag_in, sign):
    leading = real_in.shape[:-1]
    length = real_in.shape[-1]
    inner_len = 64
    outer_len = length // inner_len
    split_real = real_in.reshape(leading + (outer_len, inner_len))
    table_real, table_imag = dft_table(outer_len, sign)
    first_real = section_one(table_real, split_real)
    first_imag = section_one(table_imag, split_real)
    if imag_in is not None:
        split_imag = imag_in.reshape(leading + (outer_len, inner_len))
        first_real = first_real - section_one(table_imag, split_imag)
        first_imag = first_imag + section_one(table_real, split_imag)
    outer_index = jnp.arange(outer_len, dtype=jnp.int32)
    inner_index = jnp.arange(inner_len, dtype=jnp.int32)
    twist_phase = outer_index[:, None] * inner_index[None, :] % length
    twist_angle = 2.0 * math.pi / length * twist_phase.astype(jnp.float32)
    twist_real = jnp.cos(twist_angle)
    twist_imag = sign * jnp.sin(twist_angle)
    mid_real = first_real * twist_real - first_imag * twist_imag
    mid_imag = first_real * twist_imag + first_imag * twist_real
    last_real, last_imag = dft_table(inner_len, sign)
    out_real = section_two(last_real, mid_real) - section_two(last_imag, mid_imag)
    out_imag = section_two(last_real, mid_imag) + section_two(last_imag, mid_real)
    factor = 1.0 / math.sqrt(length)
    return (
        (out_real * factor).reshape(leading + (length,)),
        (out_imag * factor).reshape(leading + (length,)),
    )


def pieces_from_image(extrap, band_count, group_count):
    rows_dev = extrap.shape[0]
    image_width = extrap.shape[1]
    stripe = image_width // band_count
    piece_cols = stripe // group_count
    piece_rows = image_width // group_count
    col_real, col_imag = dft_last(extrap, None, -1.0)
    shaped = jnp.stack([col_real, col_imag]).reshape(
        2, 1, 1, rows_dev, band_count, group_count, piece_cols
    )
    moved = lax.all_to_all(
        lax.all_to_all(shaped, "band", split_axis=4, concat_axis=1, tiled=True),
        "vis",
        split_axis=5,
        concat_axis=2,
        tiled=True,
    )
    columns = jnp.transpose(moved.reshape(2, image_width, piece_cols), (2, 0, 1))
    row_real, row_imag = dft_last(columns[:, 0], columns[:, 1], -1.0)
    stacked = (
        jnp.stack([row_real, row_imag], axis=1)
        .astype(jnp.bfloat16)
        .reshape(piece_cols, 2, group_count, piece_rows)
    )
    pieces = lax.all_to_all(stacked, "vis", split_axis=2, concat_axis=0, tiled=True)
    return pieces.reshape(stripe, 2, piece_rows)


def image_from_pieces(piece_sum, band_count, group_count):
    stripe = piece_sum.shape[0]
    piece_rows = piece_sum.shape[2]
    piece_cols = stripe // group_count
    image_width = piece_rows * group_count
    rows_dev = image_width // (band_count * group_count)
    spread = lax.all_to_all(
        piece_sum.reshape(stripe, 2, 1, piece_rows), "vis", split_axis=0, concat_axis=2, tiled=True
    )
    spread = spread.reshape(piece_cols, 2, image_width)
    col_real, col_imag = dft_last(spread[:, 0], spread[:, 1], 1.0)
    stacked = jnp.transpose(jnp.stack([col_real, col_imag]), (0, 2, 1))
    shaped = stacked.reshape(2, band_count, group_count, rows_dev, 1, 1, piece_cols)
    moved = lax.all_to_all(
        lax.all_to_all(shaped, "band", split_axis=1, concat_axis=4, tiled=True),
        "vis",
        split_axis=2,
        concat_axis=5,
        tiled=True,
    )
    moved = moved.reshape(2, rows_dev, image_width)
    out_real, out_imag = dft_last(moved[0], moved[1], 1.0)
    return out_real


def cols_down(field):
    image_width = field.shape[1]
    extended = jnp.concatenate([field, field[:, :6]], axis=1)
    low_part = 0.0
    high_part = 0.0
    for offset in range(8):
        taken = extended[:, offset : offset + image_width : 2]
        low_part = low_part + low_taps[offset] * taken
        high_part = high_part + high_taps[offset] * taken
    return (low_part, high_part)


def cols_up(low_part, high_part):
    halves = []
    for parity in range(2):
        summed = 0.0
        for delay in range(4):
            summed = summed + low_taps[parity + 2 * delay] * jnp.roll(low_part, delay, axis=1)
            summed = summed + high_taps[parity + 2 * delay] * jnp.roll(high_part, delay, axis=1)
        halves.append(summed)
    return jnp.stack(halves, axis=2).reshape(low_part.shape[0], 2 * low_part.shape[1])


def rows_up(low_ext, high_ext, half_rows):
    halves = []
    for parity in range(2):
        summed = 0.0
        for delay in range(4):
            begin = 3 - delay
            summed = summed + low_taps[parity + 2 * delay] * low_ext[begin : begin + half_rows]
            summed = summed + high_taps[parity + 2 * delay] * high_ext[begin : begin + half_rows]
        halves.append(summed)
    return jnp.stack(halves, axis=1).reshape(2 * half_rows, low_ext.shape[1])


def analysis(extrap):
    rows_dev = extrap.shape[0]
    taken_rows = min(6, rows_dev)
    parts_list = [extrap]
    parts_list.append(shifted(extrap[:taken_rows], ("band", "vis"), -1))
    extended = jnp.concatenate(parts_list, axis=0)
    half_rows = rows_dev // 2
    rows_low = 0.0
    rows_high = 0.0
    for offset in range(8):
        taken = extended[offset : offset + 2 * half_rows : 2]
        rows_low = rows_low + low_taps[offset] * taken
        rows_high = rows_high + high_taps[offset] * taken
    low_low, low_high = cols_down(rows_low)
    high_low, high_high = cols_down(rows_high)
    return jnp.stack([low_low, low_high, high_low, high_high])


def synthesis(coef_dual):
    half_rows = coef_dual.shape[1]
    taken_rows = min(3, half_rows)
    parts_list = [shifted(coef_dual[:, half_rows - taken_rows :, :], ("band", "vis"), 1)]
    joined = jnp.concatenate(parts_list[::-1] + [coef_dual], axis=1)
    cols_low = rows_up(joined[0], joined[2], half_rows)
    cols_high = rows_up(joined[1], joined[3], half_rows)
    return cols_up(cols_low, cols_high)


def degrid(kernel_here, tiles):
    kernel_real = kernel_here[:, :, 0]
    kernel_imag = kernel_here[:, :, 1]
    tile_real = tiles[:, :, 0]
    tile_imag = tiles[:, :, 1]
    out_real = jnp.einsum(
        "qsat,qst->qsa", kernel_real, tile_real, preferred_element_type=jnp.float32
    ) - jnp.einsum("qsat,qst->qsa", kernel_imag, tile_imag, preferred_element_type=jnp.float32)
    out_imag = jnp.einsum(
        "qsat,qst->qsa", kernel_real, tile_imag, preferred_element_type=jnp.float32
    ) + jnp.einsum("qsat,qst->qsa", kernel_imag, tile_real, preferred_element_type=jnp.float32)
    return jnp.stack([out_real, out_imag], axis=2)


def grid_back(kernel_here, weights):
    kernel_real = kernel_here[:, :, 0]
    kernel_imag = kernel_here[:, :, 1]
    weight_real = weights[:, :, 0]
    weight_imag = weights[:, :, 1]
    grid_real = jnp.einsum(
        "qsat,qsa->qst", kernel_real, weight_real, preferred_element_type=jnp.float32
    ) + jnp.einsum("qsat,qsa->qst", kernel_imag, weight_imag, preferred_element_type=jnp.float32)
    grid_imag = jnp.einsum(
        "qsat,qsa->qst", kernel_real, weight_imag, preferred_element_type=jnp.float32
    ) - jnp.einsum("qsat,qsa->qst", kernel_imag, weight_real, preferred_element_type=jnp.float32)
    return jnp.stack([grid_real, grid_imag], axis=2)


def local(sky_image, coef_dual, vis_dual, visibilities, kernel_blocks, tile_rows, tile_counts):
    band_count = lax.axis_size("band")
    group_count = lax.axis_size("vis")
    kernel_here = kernel_blocks[0, 0]
    rows_here = tile_rows[0, 0]
    slot_count = rows_here.shape[1]
    live_slots = (
        jnp.arange(slot_count, dtype=jnp.int32)[None, :] < tile_counts[0, 0][:, None]
    ).astype(jnp.float32)[:, :, None, None]
    vis_data = visibilities[0, 0]
    vis_state = vis_dual[0, 0]
    image_width = sky_image.shape[1]
    stripe = image_width // band_count
    piece_rows = image_width // group_count
    incoming_rows = lax.all_to_all(rows_here, "vis", split_axis=0, concat_axis=0, tiled=True)
    data_part = jnp.sum(live_slots * vis_data * vis_data)
    weights = (live_slots * vis_state).astype(jnp.bfloat16)
    contrib = grid_back(kernel_here, weights)
    arrived = lax.all_to_all(contrib, "vis", split_axis=0, concat_axis=0, tiled=True)
    piece_sum = jax.ops.segment_sum(
        arrived.reshape(-1, 2, piece_rows), incoming_rows.reshape(-1), num_segments=stripe
    )
    adjoint_part = image_from_pieces(piece_sum, band_count, group_count)
    smooth = synthesis(coef_dual)
    new_image = jnp.maximum(sky_image - smooth - adjoint_part, 0.0)
    extrap = 2.0 * new_image - sky_image
    coeffs = analysis(extrap)
    abs_total = jnp.sum(jnp.abs(coeffs))
    coef_total = lax.psum(abs_total, ("band", "vis"))
    threshold = 0.5 * coef_total / (IMG * IMG)
    coef_dual = jnp.clip(coef_dual + coeffs, -threshold, threshold)
    piece_grid = pieces_from_image(extrap, band_count, group_count)
    tiles = lax.all_to_all(
        piece_grid[incoming_rows], "vis", split_axis=0, concat_axis=0, tiled=True
    )
    predicted = degrid(kernel_here, tiles)
    residual = live_slots * (vis_state + predicted - vis_data)
    resid_square = jnp.sum(residual * residual)
    norm_square, data_square = lax.psum((resid_square, data_part), ("band", "vis"))
    radius = 0.5 * jnp.sqrt(data_square + 1e-06)
    size_value = jnp.sqrt(norm_square + 1e-06)
    vis_state = residual * (1.0 - jnp.minimum(1.0, radius / size_value))
    return (new_image, coef_dual, vis_state[None, None])


def solution(mesh):
    return jax.shard_map(
        local,
        mesh=mesh,
        in_specs=(
            P(("band", "vis"), None),
            P(None, ("band", "vis"), None),
            P("band", "vis", None, None, None, None),
            P("band", "vis", None, None, None, None),
            P("band", "vis", None, None, None, None, None),
            P("band", "vis", None, None),
            P("band", "vis", None),
        ),
        out_specs=(
            P(("band", "vis"), None),
            P(None, ("band", "vis"), None),
            P("band", "vis", None, None, None, None),
        ),
        check_vma=False,
    )
```

profile of v0, /device:TPU:0, one launch (start us, length us, event | category | flops | bytes accessed | tf_op | source)
XLA Modules:
  0.0 1030.4 jit_solution(3161300191963925182)
XLA Ops:
  2.1 7.4 all-to-all-start
  15.9 5.8 all-to-all-start.1
  23.0 6.6 all-to-all-done.1
  32.6 7.0 scatter_fusion
  44.6 77.0 %all-to-all-done.2 = f32[2048,2,1,256]{3,1,2,0:T(2,128)} async-done(((f32[2048,2,1,256]{3,1,2,0:T(2,128)}), f32[2048,2,1,256]{3,1,2,0:T(2,128)}, u32[]{:S(2)}, u32[]{:S(2)}) %all-to-all-start.2) | async-done | bytes 4194336 | tf_op jit(solution)/shard_map/all_to_all | solution.py:108
  121.6 4.6 copy.230
  126.2 5.8 copy.231
  167.5 5.4 copy.244
  172.9 52.8 %all_to_all.118 = f32[2,2,16,128,1,1,128]{3,6,2,0,5,4,1:T(8,128)S(1)} all-to-all(f32[2,2,16,128,1,1,128]{3,6,2,0,5,4,1:T(8,128)} %copy.244), channel_id=1, replica_groups=mesh['band'=2,'vis'=16] {'band'}, dimensions={1} | all-to-all | bytes 8388608 | tf_op jit(solution)/shard_map/all_to_all | solution.py:116
  228.0 19.2 %all-to-all-start.4 = ((f32[2,1,16,128,2,1,128]{3,6,4,0,5,1,2:T(8,128)}), f32[2,1,16,128,2,1,128]{3,6,4,0,5,1,2:T(8,128)}, u32[]{:S(2)}, u32[]{:S(2)}) async-start(f32[2,1,16,128,2,1,128]{3,6,4,0,5,1,2:T(8,128)} %copy.245), calls=%async_computation.4 | async-start | bytes 8388608 | tf_op jit(solution)/shard_map/all_to_all | solution.py:115
  250.8 71.3 %collective-permute-done = f32[4,3,2048]{2,1,0:T(4,128)S(1)} collective-permute-done((f32[4,3,2048]{2,1,0:T(4,128)S(1)}, f32[4,3,2048]{2,1,0:T(4,128)S(1)}, u32[]{:S(2)}, u32[]{:S(2)}) %collective-permute-start) | collective-permute-done | bytes 98336 | tf_op jit(solution)/shard_map/ppermute | solution.py:25
  402.0 29.7 %all_to_all.119 = f32[2,1,1,128,2,16,128]{3,6,5,2,1,0,4:T(8,128)S(1)} all-to-all(f32[2,1,1,128,2,16,128]{3,6,5,2,1,0,4:T(8,128)S(1)} %copy.267), channel_id=1, replica_groups=mesh['band'=2,'vis'=16] {'band'}, dimensions={4} | all-to-all | bytes 8388608 | tf_op jit(solution)/shard_map/all_to_all | solution.py:85
  434.0 22.5 %all-to-all-start.6 = ((f32[2,2,1,128,1,16,128]{3,6,1,0,4,2,5:T(8,128)}), f32[2,2,1,128,1,16,128]{3,6,1,0,4,2,5:T(8,128)}, u32[]{:S(2)}, u32[]{:S(2)}) async-start(f32[2,2,1,128,1,16,128]{3,6,1,0,4,2,5:T(8,128)} %copy.268), calls=%async_computation.6 | async-start | bytes 8388608 | tf_op jit(solution)/shard_map/all_to_all | solution.py:84
  465.0 41.1 %slice.319 = f32[64,4096]{0,1:T(8,128)} slice(f32[128,4096]{0,1:T(8,128)S(1)} %get-tuple-element.20), slice={[0:128:2], [0:4096:1]} | slice | bytes 2097152 | tf_op jit(solution)/shard_map/slice | solution.py:172
  509.0 17.5 %collective-permute-done.1 = f32[6,4096]{1,0:T(8,128)S(1)} collective-permute-done((f32[6,4096]{1,0:T(8,128)S(1)}, f32[6,4096]{1,0:T(8,128)S(1)}, u32[]{:S(2)}, u32[]{:S(2)}) %collective-permute-start.1) | collective-permute-done | bytes 98336 | tf_op jit(solution)/shard_map/ppermute | solution.py:25
  532.3 39.0 %slice.321 = f32[64,4096]{0,1:T(8,128)} slice(f32[134,4096]{0,1:T(8,128)} %pad_maximum_fusion.1), slice={[1:129:2], [0:4096:1]} | slice | bytes 2097152 | tf_op jit(solution)/shard_map/slice | solution.py:172
  571.2 39.0 %slice.322 = f32[64,4096]{0,1:T(8,128)} slice(f32[134,4096]{0,1:T(8,128)} %pad_maximum_fusion.1), slice={[2:130:2], [0:4096:1]} | slice | bytes 2097152 | tf_op jit(solution)/shard_map/slice | solution.py:172
  610.2 39.0 %slice.323 = f32[64,4096]{0,1:T(8,128)} slice(f32[134,4096]{0,1:T(8,128)} %pad_maximum_fusion.1), slice={[3:131:2], [0:4096:1]} | slice | bytes 2097152 | tf_op jit(solution)/shard_map/slice | solution.py:172
  649.2 39.0 %slice.324 = f32[64,4096]{0,1:T(8,128)} slice(f32[134,4096]{0,1:T(8,128)} %pad_maximum_fusion.1), slice={[4:132:2], [0:4096:1]} | slice | bytes 2097152 | tf_op jit(solution)/shard_map/slice | solution.py:172
  688.1 39.0 %slice.325 = f32[64,4096]{0,1:T(8,128)} slice(f32[134,4096]{0,1:T(8,128)} %pad_maximum_fusion.1), slice={[5:133:2], [0:4096:1]} | slice | bytes 2097152 | tf_op jit(solution)/shard_map/slice | solution.py:172
  727.1 39.0 %slice.326 = f32[64,4096]{0,1:T(8,128)} slice(f32[134,4096]{0,1:T(8,128)} %pad_maximum_fusion.1), slice={[6:134:2], [0:4096:1]} | slice | bytes 2097152 | tf_op jit(solution)/shard_map/slice | solution.py:172
  766.0 39.0 %slice.327 = f32[64,4096]{0,1:T(8,128)} slice(f32[134,4096]{0,1:T(8,128)} %pad_maximum_fusion.1), slice={[7:134:2], [0:4096:1]} | slice | bytes 2097152 | tf_op jit(solution)/shard_map/slice | solution.py:172
  805.0 5.5 copy.269
  823.0 4.8 fusion
  844.7 27.9 %all-to-all-start.7 = ((bf16[128,2,16,256]{0,3,1,2:T(8,128)(2,1)}), bf16[128,2,16,256]{0,3,1,2:T(8,128)(2,1)}, u32[]{:S(2)}, u32[]{:S(2)}) async-start(bf16[128,2,16,256]{0,3,1,2:T(8,128)(2,1)} %copy.280), calls=%async_computation.7 | async-start | bytes 4194304 | tf_op jit(solution)/shard_map/all_to_all | solution.py:98
  872.6 7.4 multiply_add_fusion.1
  903.2 6.2 slice.328
  936.1 6.2 slice.337
  953.9 5.8 copy.284
  962.6 6.0 all-to-all-start.8
  980.6 38.1 %all-reduce = (f32[]{:T(128)}, f32[]{:T(128)}, f32[]{:T(128)}) all-reduce(f32[]{:T(128)} %abs_reduce_fusion, f32[]{:T(128)} %get-tuple-element.16, f32[]{:T(128)} %get-tuple-element.15), channel_id=1, replica_groups=mesh['band'=2,'vis'=16] {'band','vis'}, use_global_device_ids=true, to_apply=%region_2.3 | all-reduce | flops 3 | bytes 24 | tf_op jit(solution)/shard_map/psum | solution.py:246
  1020.6 5.0 maximum_minimum_fusion
  (185 shorter events, 267.4 us)
Async XLA Ops:
  0.6 13.6 %copy-start.18 = (bf16[1,1,16,4,2,32,256]{6,5,4,3,2,1,0:T(8,128)(2,1)S(1)}, bf16[1,1,16,4,2,32,256]{6,5,4,3,2,1,0:T(8,128)(2,1)}, u32[]{:S(2)}) copy-start(bf16[1,1,16,4,2,32,256]{6,5,4,3,2,1,0:T(8,128)(2,1)} %param.11) | copy-start | bytes 6291460
  2.1 13.8 %all-to-all-start = ((s32[16,1,4]{2,1,0:T(1,128)}), s32[16,1,4]{2,1,0:T(1,128)S(1)}, u32[]{:S(2)}, u32[]{:S(2)}) async-start(s32[16,1,4]{2,1,0:T(1,128)} %copy.227), calls=%async_computation | async-start | bytes 16384 | tf_op jit(solution)/shard_map/all_to_all | solution.py:232
  10.3 1.0 copy-start.16
  15.9 13.7 %all-to-all-start.1 = ((f32[16,4,2,256]{3,2,1,0:T(2,128)}), f32[16,4,2,256]{3,2,1,0:T(2,128)S(1)}, u32[]{:S(2)}, u32[]{:S(2)}) async-start(f32[16,4,2,256]{3,2,1,0:T(2,128)} %pad_maximum_fusion.17), calls=%async_computation.1 | async-start | bytes 262144 | tf_op jit(solution)/shard_map/all_to_all | solution.py:236
  39.6 82.0 %all-to-all-start.2 = ((f32[2048,2,1,256]{3,1,2,0:T(2,128)}), f32[2048,2,1,256]{3,1,2,0:T(2,128)}, u32[]{:S(2)}, u32[]{:S(2)}) async-start(f32[2048,2,1,256]{3,1,2,0:T(2,128)} %bitcast.318), calls=%async_computation.2 | async-start | bytes 8388608 | tf_op jit(solution)/shard_map/all_to_all | solution.py:108
  228.0 19.2 %copy-start = (f32[4,64,2048]{2,1,0:T(8,128)S(1)}, f32[4,64,2048]{2,1,0:T(8,128)}, u32[]{:S(2)}) copy-start(f32[4,64,2048]{2,1,0:T(8,128)} %param.8) | copy-start | bytes 6291460
  228.0 120.3 %all-to-all-start.4 = ((f32[2,1,16,128,2,1,128]{3,6,4,0,5,1,2:T(8,128)}), f32[2,1,16,128,2,1,128]{3,6,4,0,5,1,2:T(8,128)}, u32[]{:S(2)}, u32[]{:S(2)}) async-start(f32[2,1,16,128,2,1,128]{3,6,4,0,5,1,2:T(8,128)} %copy.245), calls=%async_computation.4 | async-start | bytes 8388608 | tf_op jit(solution)/shard_map/all_to_all | solution.py:115
  247.3 74.8 %collective-permute-start = (f32[4,3,2048]{2,1,0:T(4,128)S(1)}, f32[4,3,2048]{2,1,0:T(4,128)S(1)}, u32[]{:S(2)}, u32[]{:S(2)}) collective-permute-start(f32[4,3,2048]{2,1,0:T(4,128)S(1)} %slice.284), channel_id=1, source_target_pairs={{31,0},{0,1},{1,2},{2,3},{3,4},{4,5},{5,6},{6,7},{7,8},{8,9},{9,10... | collective-permute-start | bytes 294920 | tf_op jit(solution)/shard_map/ppermute | solution.py:25
  342.2 1.7 copy-start.5
  372.6 1.6 copy-start.2
  372.6 2.2 copy-start.4
  434.0 371.0 %all-to-all-start.6 = ((f32[2,2,1,128,1,16,128]{3,6,1,0,4,2,5:T(8,128)}), f32[2,2,1,128,1,16,128]{3,6,1,0,4,2,5:T(8,128)}, u32[]{:S(2)}, u32[]{:S(2)}) async-start(f32[2,2,1,128,1,16,128]{3,6,1,0,4,2,5:T(8,128)} %copy.268), calls=%async_computation.6 | async-start | bytes 8388608 | tf_op jit(solution)/shard_map/all_to_all | solution.py:84
  461.2 65.2 %collective-permute-start.1 = (f32[6,4096]{1,0:T(8,128)S(1)}, f32[6,4096]{1,0:T(8,128)S(1)}, u32[]{:S(2)}, u32[]{:S(2)}) collective-permute-start(f32[6,4096]{1,0:T(8,128)S(1)} %copy.255), channel_id=1, source_target_pairs={{1,0},{2,1},{3,2},{4,3},{5,4},{6,5},{7,6},{8,7},{9,8},{10,9},{11,1... | collective-permute-start | bytes 294920 | tf_op jit(solution)/shard_map/ppermute | solution.py:25
  844.7 27.9 %copy-start.3 = (f32[64,4096]{0,1:T(8,128)S(1)}, f32[64,4096]{0,1:T(8,128)}, u32[]{:S(2)}) copy-start(f32[64,4096]{0,1:T(8,128)} %slice.319) | copy-start | bytes 3145732
  844.7 105.3 %all-to-all-start.7 = ((bf16[128,2,16,256]{0,3,1,2:T(8,128)(2,1)}), bf16[128,2,16,256]{0,3,1,2:T(8,128)(2,1)}, u32[]{:S(2)}, u32[]{:S(2)}) async-start(bf16[128,2,16,256]{0,3,1,2:T(8,128)(2,1)} %copy.280), calls=%async_computation.7 | async-start | bytes 4194304 | tf_op jit(solution)/shard_map/all_to_all | solution.py:98
  880.0 1.4 copy-start.1
  942.3 4.4 copy-start.6
  942.3 4.4 copy-start.7
  942.3 4.4 copy-start.8
  942.3 4.4 copy-start.9
  942.3 4.7 copy-start.10
  942.3 5.0 copy-start.11
  942.3 5.3 copy-start.12
  942.4 5.5 copy-start.13
  962.6 12.9 %all-to-all-start.8 = ((bf16[16,4,2,256]{3,2,1,0:T(2,128)(2,1)}), bf16[16,4,2,256]{3,2,1,0:T(2,128)(2,1)S(1)}, u32[]{:S(2)}, u32[]{:S(2)}) async-start(bf16[16,4,2,256]{3,2,1,0:T(2,128)(2,1)} %bitcast.95), calls=%async_computation.8 | async-start | bytes 131072 | tf_op jit(solution)/shard_map/all_to_all | solution.py:250
  975.5 3.5 copy-start.19
  977.3 2.5 copy-start.14
  977.3 2.5 copy-start.15
  977.3 2.5 copy-start.17
where the time goes:
time: 1040 us; the launch traced here: 1030 us
  local copies, waits for them, and re-layouts  472 us (45%)
  waiting for transfers between devices  177 us (17%)
  blocking collectives  121 us (12%)
  matrix products  108 us (10%)
  starting transfers between devices  97.5 us (9%)
  other arithmetic  51.8 us (5%)
    slice x8, local copies, waits for them, and re-layouts, analysis(): taken = extended[offset:offset + 2 * half_rows:2]  314 us
    ppermute x2, waiting for transfers between devices, shifted(): return lax.ppermute(block, axis, route)  88.9 us
    all_to_all x1, waiting for transfers between devices, image_from_pieces(): lax.all_to_all(piece_sum.reshape(stripe, 2, 1, piece_rows), 'vis', split_...  77 us
    slice x16, local copies, waits for them, and re-layouts, cols_down(): taken = extended[:, offset:offset + image_width:2]  58.4 us
    all_to_all x1, blocking collectives, image_from_pieces(): lax.all_to_all(shaped, 'band', split_axis=1, concat_axis=4, tiled=True)  52.8 us
    dot_general x14, matrix products, section_one(): return jnp.einsum('kn,...nm->...km', table, values, precision=highest)  51.9 us
    dot_general x14, matrix products, section_two(): return jnp.einsum('qm,...km->...qk', table, values, precision=highest)  48.1 us
    psum x1, blocking collectives, local(): coef_total = lax.psum(abs_total, ('band', 'vis'))  38.1 us
  transfers between devices with their start and end apart: 9, of which 6 were waited for; matrix products, arithmetic and copies ran while one was open for 43% of the time, Pallas kernels for 0%

commit v1 on v0

--- a/solution.py
+++ b/solution.py
@@ -3,6 +3,7 @@
 import jax.numpy as jnp
 from jax import lax
 from jax.sharding import PartitionSpec as P
+from jax.lax import all_to_all, psum
 
 IMG = 4096
 low_taps = (
@@ -81,12 +82,15 @@
     shaped = jnp.stack([col_real, col_imag]).reshape(
         2, 1, 1, rows_dev, band_count, group_count, piece_cols
     )
-    moved = lax.all_to_all(
-        lax.all_to_all(shaped, "band", split_axis=4, concat_axis=1, tiled=True),
-        "vis",
-        split_axis=5,
-        concat_axis=2,
-        tiled=True,
+
+    def _note_tiles(patch, named_axis):
+        small = jnp.split(patch, psum(1, named_axis), axis=5)
+        y_new = jnp.stack(small)
+        d_next = all_to_all(y_new, named_axis, 0, 0)
+        return jnp.concatenate(d_next, axis=2)
+
+    moved = _note_tiles(
+        lax.all_to_all(shaped, "band", split_axis=4, concat_axis=1, tiled=True), "vis"
     )
     columns = jnp.transpose(moved.reshape(2, image_width, piece_cols), (2, 0, 1))
     row_real, row_imag = dft_last(columns[:, 0], columns[:, 1], -1.0)

time: 1040 us -> 1050 us (level)
    unnamed x46 -> x61, local copies, waits for them, and re-layouts: 16.9 us -> 27.7 us
  transfers between devices with their start and end apart: 9 -> 9, of which waited for: 6 -> 6; matrix products, arithmetic and copies ran while one was open for 43% -> 42% of each run, Pallas kernels for 0% -> 0%
where the time goes in v1:
time: 1050 us; the launch traced here: 1040 us
  local copies, waits for them, and re-layouts  482 us (46%)
  waiting for transfers between devices  177 us (17%)
  blocking collectives  121 us (12%)
  matrix products  108 us (10%)
  starting transfers between devices  97.9 us (9%)
  other arithmetic  51.6 us (5%)
    slice x8, local copies, waits for them, and re-layouts, analysis(): taken = extended[offset:offset + 2 * half_rows:2]  314 us
    ppermute x2, waiting for transfers between devices, shifted(): return lax.ppermute(block, axis, route)  89.1 us
    all_to_all x1, waiting for transfers between devices, image_from_pieces(): lax.all_to_all(piece_sum.reshape(stripe, 2, 1, piece_rows), 'vis', split_...  77 us
    slice x16, local copies, waits for them, and re-layouts, cols_down(): taken = extended[:, offset:offset + image_width:2]  58.4 us
    all_to_all x1, blocking collectives, image_from_pieces(): lax.all_to_all(shaped, 'band', split_axis=1, concat_axis=4, tiled=True)  52.8 us
    dot_general x14, matrix products, section_one(): return jnp.einsum('kn,...nm->...km', table, values, precision=highest)  51.6 us
    dot_general x14, matrix products, section_two(): return jnp.einsum('qm,...km->...qk', table, values, precision=highest)  48.5 us
    psum x1, blocking collectives, local(): coef_total = lax.psum(abs_total, ('band', 'vis'))  38.1 us
  transfers between devices with their start and end apart: 9, of which 6 were waited for; matrix products, arithmetic and copies ran while one was open for 42% of the time, Pallas kernels for 0%

profile of v1, /device:TPU:0, one launch (start us, length us, event | category | flops | bytes accessed | tf_op | source)
XLA Modules:
  0.0 1040.1 jit_solution(16964855754754853718)
XLA Ops:
  2.1 7.4 all-to-all-start
  15.9 5.8 all-to-all-start.1
  23.0 6.6 all-to-all-done.1
  32.6 7.0 scatter_fusion
  44.6 77.0 %all-to-all-done.2 = f32[2048,2,1,256]{3,1,2,0:T(2,128)} async-done(((f32[2048,2,1,256]{3,1,2,0:T(2,128)}), f32[2048,2,1,256]{3,1,2,0:T(2,128)}, u32[]{:S(2)}, u32[]{:S(2)}) %all-to-all-start.2) | async-done | bytes 4194336 | tf_op jit(solution)/shard_map/all_to_all | solution.py:112
  126.2 5.5 copy.377
  144.2 4.6 fusion.7
  167.5 5.4 copy.390
  172.8 52.8 %all_to_all.108 = f32[2,2,16,128,1,1,128]{3,6,2,0,5,4,1:T(8,128)S(1)} all-to-all(f32[2,2,16,128,1,1,128]{3,6,2,0,5,4,1:T(8,128)} %copy.390), channel_id=1, replica_groups=mesh['band'=2,'vis'=16] {'band'}, dimensions={1} | all-to-all | bytes 8388608 | tf_op jit(solution)/shard_map/all_to_all | solution.py:120
  228.0 19.2 %all-to-all-start.4 = ((f32[2,1,16,128,2,1,128]{3,6,4,0,5,1,2:T(8,128)}), f32[2,1,16,128,2,1,128]{3,6,4,0,5,1,2:T(8,128)}, u32[]{:S(2)}, u32[]{:S(2)}) async-start(f32[2,1,16,128,2,1,128]{3,6,4,0,5,1,2:T(8,128)} %copy.391), calls=%async_computation.4 | async-start | bytes 8388608 | tf_op jit(solution)/shard_map/all_to_all | solution.py:119
  250.8 71.3 %collective-permute-done = f32[4,3,2048]{2,1,0:T(4,128)S(1)} collective-permute-done((f32[4,3,2048]{2,1,0:T(4,128)S(1)}, f32[4,3,2048]{2,1,0:T(4,128)S(1)}, u32[]{:S(2)}, u32[]{:S(2)}) %collective-permute-start) | collective-permute-done | bytes 98336 | tf_op jit(solution)/shard_map/ppermute | solution.py:26
  361.0 4.7 fusion.5
  401.9 29.7 %all_to_all.109 = f32[2,1,1,128,2,16,128]{3,6,5,2,1,0,4:T(8,128)S(1)} all-to-all(f32[2,1,1,128,2,16,128]{3,6,5,2,1,0,4:T(8,128)S(1)} %copy.413), channel_id=1, replica_groups=mesh['band'=2,'vis'=16] {'band'}, dimensions={4} | all-to-all | bytes 8388608 | tf_op jit(solution)/shard_map/all_to_all | solution.py:93
  443.1 5.5 copy.429
  448.6 22.7 %all-to-all-start.6 = ((f32[16,2,2,1,128,1,1,128]{7,4,2,1,6,5,3,0:T(8,128)}), f32[16,2,2,1,128,1,1,128]{7,4,2,1,6,5,3,0:T(8,128)}, u32[]{:S(2)}, u32[]{:S(2)}) async-start(f32[16,2,2,1,128,1,1,128]{7,4,2,1,6,5,3,0:T(8,128)} %copy.429), calls=%async_computation.6 | async-start | bytes 8388608 | tf_op jit(solution)/shard_map/all_to_all | solution.py:89
  479.9 40.7 %slice.319 = f32[64,4096]{0,1:T(8,128)} slice(f32[128,4096]{0,1:T(8,128)S(1)} %get-tuple-element.23), slice={[0:128:2], [0:4096:1]} | slice | bytes 2097152 | tf_op jit(solution)/shard_map/slice | solution.py:176
  523.5 17.7 %collective-permute-done.1 = f32[6,4096]{1,0:T(8,128)S(1)} collective-permute-done((f32[6,4096]{1,0:T(8,128)S(1)}, f32[6,4096]{1,0:T(8,128)S(1)}, u32[]{:S(2)}, u32[]{:S(2)}) %collective-permute-start.1) | collective-permute-done | bytes 98336 | tf_op jit(solution)/shard_map/ppermute | solution.py:26
  547.0 39.0 %slice.321 = f32[64,4096]{0,1:T(8,128)} slice(f32[134,4096]{0,1:T(8,128)} %pad_maximum_fusion.1), slice={[1:129:2], [0:4096:1]} | slice | bytes 2097152 | tf_op jit(solution)/shard_map/slice | solution.py:176
  586.0 39.0 %slice.322 = f32[64,4096]{0,1:T(8,128)} slice(f32[134,4096]{0,1:T(8,128)} %pad_maximum_fusion.1), slice={[2:130:2], [0:4096:1]} | slice | bytes 2097152 | tf_op jit(solution)/shard_map/slice | solution.py:176
  624.9 39.0 %slice.323 = f32[64,4096]{0,1:T(8,128)} slice(f32[134,4096]{0,1:T(8,128)} %pad_maximum_fusion.1), slice={[3:131:2], [0:4096:1]} | slice | bytes 2097152 | tf_op jit(solution)/shard_map/slice | solution.py:176
  663.9 39.0 %slice.324 = f32[64,4096]{0,1:T(8,128)} slice(f32[134,4096]{0,1:T(8,128)} %pad_maximum_fusion.1), slice={[4:132:2], [0:4096:1]} | slice | bytes 2097152 | tf_op jit(solution)/shard_map/slice | solution.py:176
  702.8 39.0 %slice.325 = f32[64,4096]{0,1:T(8,128)} slice(f32[134,4096]{0,1:T(8,128)} %pad_maximum_fusion.1), slice={[5:133:2], [0:4096:1]} | slice | bytes 2097152 | tf_op jit(solution)/shard_map/slice | solution.py:176
  741.8 39.0 %slice.326 = f32[64,4096]{0,1:T(8,128)} slice(f32[134,4096]{0,1:T(8,128)} %pad_maximum_fusion.1), slice={[6:134:2], [0:4096:1]} | slice | bytes 2097152 | tf_op jit(solution)/shard_map/slice | solution.py:176
  780.8 39.4 %slice.327 = f32[64,4096]{0,1:T(8,128)} slice(f32[134,4096]{0,1:T(8,128)} %pad_maximum_fusion.1), slice={[7:134:2], [0:4096:1]} | slice | bytes 2097152 | tf_op jit(solution)/shard_map/slice | solution.py:176
  854.3 27.9 %all-to-all-start.7 = ((bf16[128,2,16,256]{0,3,1,2:T(8,128)(2,1)}), bf16[128,2,16,256]{0,3,1,2:T(8,128)(2,1)}, u32[]{:S(2)}, u32[]{:S(2)}) async-start(bf16[128,2,16,256]{0,3,1,2:T(8,128)(2,1)} %copy.441), calls=%async_computation.7 | async-start | bytes 4194304 | tf_op jit(solution)/shard_map/all_to_all | solution.py:102
  882.2 7.4 multiply_add_fusion.1
  912.8 6.2 slice.328
  945.7 6.2 slice.337
  963.5 5.8 copy.445
  972.2 6.0 all-to-all-start.8
  990.3 38.1 %all-reduce = (f32[]{:T(128)}, f32[]{:T(128)}, f32[]{:T(128)}) all-reduce(f32[]{:T(128)} %abs_reduce_fusion, f32[]{:T(128)} %get-tuple-element.19, f32[]{:T(128)} %get-tuple-element.18), channel_id=1, replica_groups=mesh['band'=2,'vis'=16] {'band','vis'}, use_global_device_ids=true, to_apply=%region_2.3 | all-reduce | flops 3 | bytes 24 | tf_op jit(solution)/shard_map/psum | solution.py:250
  1030.3 5.0 maximum_minimum_fusion
  (201 shorter events, 277.0 us)
Async XLA Ops:
  0.6 13.6 %copy-start.18 = (bf16[1,1,16,4,2,32,256]{6,5,4,3,2,1,0:T(8,128)(2,1)S(1)}, bf16[1,1,16,4,2,32,256]{6,5,4,3,2,1,0:T(8,128)(2,1)}, u32[]{:S(2)}) copy-start(bf16[1,1,16,4,2,32,256]{6,5,4,3,2,1,0:T(8,128)(2,1)} %param.11) | copy-start | bytes 6291460
  2.1 13.8 %all-to-all-start = ((s32[16,1,4]{2,1,0:T(1,128)}), s32[16,1,4]{2,1,0:T(1,128)S(1)}, u32[]{:S(2)}, u32[]{:S(2)}) async-start(s32[16,1,4]{2,1,0:T(1,128)} %copy.373), calls=%async_computation | async-start | bytes 16384 | tf_op jit(solution)/shard_map/all_to_all | solution.py:236
  10.3 1.0 copy-start.16
  15.9 13.7 %all-to-all-start.1 = ((f32[16,4,2,256]{3,2,1,0:T(2,128)}), f32[16,4,2,256]{3,2,1,0:T(2,128)S(1)}, u32[]{:S(2)}, u32[]{:S(2)}) async-start(f32[16,4,2,256]{3,2,1,0:T(2,128)} %pad_maximum_fusion.17), calls=%async_computation.1 | async-start | bytes 262144 | tf_op jit(solution)/shard_map/all_to_all | solution.py:240
  39.6 82.0 %all-to-all-start.2 = ((f32[2048,2,1,256]{3,1,2,0:T(2,128)}), f32[2048,2,1,256]{3,1,2,0:T(2,128)}, u32[]{:S(2)}, u32[]{:S(2)}) async-start(f32[2048,2,1,256]{3,1,2,0:T(2,128)} %bitcast.410), calls=%async_computation.2 | async-start | bytes 8388608 | tf_op jit(solution)/shard_map/all_to_all | solution.py:112
  228.0 19.2 %copy-start = (f32[4,64,2048]{2,1,0:T(8,128)S(1)}, f32[4,64,2048]{2,1,0:T(8,128)}, u32[]{:S(2)}) copy-start(f32[4,64,2048]{2,1,0:T(8,128)} %param.8) | copy-start | bytes 6291460
  228.0 120.1 %all-to-all-start.4 = ((f32[2,1,16,128,2,1,128]{3,6,4,0,5,1,2:T(8,128)}), f32[2,1,16,128,2,1,128]{3,6,4,0,5,1,2:T(8,128)}, u32[]{:S(2)}, u32[]{:S(2)}) async-start(f32[2,1,16,128,2,1,128]{3,6,4,0,5,1,2:T(8,128)} %copy.391), calls=%async_computation.4 | async-start | bytes 8388608 | tf_op jit(solution)/shard_map/all_to_all | solution.py:119
  247.2 74.8 %collective-permute-start = (f32[4,3,2048]{2,1,0:T(4,128)S(1)}, f32[4,3,2048]{2,1,0:T(4,128)S(1)}, u32[]{:S(2)}, u32[]{:S(2)}) collective-permute-start(f32[4,3,2048]{2,1,0:T(4,128)S(1)} %slice.284), channel_id=1, source_target_pairs={{31,0},{0,1},{1,2},{2,3},{3,4},{4,5},{5,6},{6,7},{7,8},{8,9},{9,10... | collective-permute-start | bytes 294920 | tf_op jit(solution)/shard_map/ppermute | solution.py:26
  341.9 1.7 copy-start.5
  372.6 1.6 copy-start.2
  372.6 2.2 copy-start.4
  448.6 371.6 %all-to-all-start.6 = ((f32[16,2,2,1,128,1,1,128]{7,4,2,1,6,5,3,0:T(8,128)}), f32[16,2,2,1,128,1,1,128]{7,4,2,1,6,5,3,0:T(8,128)}, u32[]{:S(2)}, u32[]{:S(2)}) async-start(f32[16,2,2,1,128,1,1,128]{7,4,2,1,6,5,3,0:T(8,128)} %copy.429), calls=%async_computation.6 | async-start | bytes 8388608 | tf_op jit(solution)/shard_map/all_to_all | solution.py:89
  476.0 65.2 %collective-permute-start.1 = (f32[6,4096]{1,0:T(8,128)S(1)}, f32[6,4096]{1,0:T(8,128)S(1)}, u32[]{:S(2)}, u32[]{:S(2)}) collective-permute-start(f32[6,4096]{1,0:T(8,128)S(1)} %copy.401), channel_id=1, source_target_pairs={{1,0},{2,1},{3,2},{4,3},{5,4},{6,5},{7,6},{8,7},{9,8},{10,9},{11,1... | collective-permute-start | bytes 294920 | tf_op jit(solution)/shard_map/ppermute | solution.py:26
  854.3 27.9 %copy-start.3 = (f32[64,4096]{0,1:T(8,128)S(1)}, f32[64,4096]{0,1:T(8,128)}, u32[]{:S(2)}) copy-start(f32[64,4096]{0,1:T(8,128)} %slice.319) | copy-start | bytes 3145732
  854.3 105.3 %all-to-all-start.7 = ((bf16[128,2,16,256]{0,3,1,2:T(8,128)(2,1)}), bf16[128,2,16,256]{0,3,1,2:T(8,128)(2,1)}, u32[]{:S(2)}, u32[]{:S(2)}) async-start(bf16[128,2,16,256]{0,3,1,2:T(8,128)(2,1)} %copy.441), calls=%async_computation.7 | async-start | bytes 4194304 | tf_op jit(solution)/shard_map/all_to_all | solution.py:102
  889.6 1.4 copy-start.1
  951.9 4.4 copy-start.6
  952.0 4.4 copy-start.7
  952.0 4.4 copy-start.8
  952.0 4.4 copy-start.9
  952.0 4.7 copy-start.10
  952.0 5.0 copy-start.11
  952.0 5.3 copy-start.12
  952.0 5.5 copy-start.13
  972.2 12.9 %all-to-all-start.8 = ((bf16[16,4,2,256]{3,2,1,0:T(2,128)(2,1)}), bf16[16,4,2,256]{3,2,1,0:T(2,128)(2,1)S(1)}, u32[]{:S(2)}, u32[]{:S(2)}) async-start(bf16[16,4,2,256]{3,2,1,0:T(2,128)(2,1)} %bitcast.111), calls=%async_computation.8 | async-start | bytes 131072 | tf_op jit(solution)/shard_map/all_to_all | solution.py:254
  985.1 3.5 copy-start.19
  986.9 2.5 copy-start.14
  987.0 2.5 copy-start.15
  987.0 2.5 copy-start.17
